TPU v7x, 32 devices: a whole 2x2x4 slice. The times are simulated.
32 devices in a mesh: blk: 8 (over y, x, core), uly: 4 (over z).
Axes of the slice: x: 2, y: 2, z: 4, core: 2. Of those that a mesh axis runs over, the one named last changes fastest.
Arguments:
- queries: bfloat16 [4096, 4096], P(('blk', 'uly')), may hold values from -128 to 128
- keys: bfloat16 [4096, 1024], P(('blk', 'uly')), may hold values from -7 to 7
- values: bfloat16 [4096, 1024], P(('blk', 'uly')), may hold values from -6 to 6
- doc_ids: int32 [4096], P(('blk', 'uly')), may hold values from 0 to 31, never falling along the last dimension, each value on 1 to 512 neighbouring positions
- out_weight: bfloat16 [4096, 4096], P('uly'), may hold values from -0.09375 to 0.09375
Outputs:
- mixed: bfloat16 [4096, 4096], P(('blk', 'uly'))
Inputs may be any that keep to these rules, and one draw needn't show every extreme that they name: `doc_ids`: document numbers never fall along the pack; each document holds 1 to 512 consecutive tokens, and some document holds exactly 512.
All inputs are finite; a program needn't handle non-finite values.
Results may differ from a plain program's by a relative error of at most 0.017.
Values may be sent and summed in bfloat16 or wider, within the bound.
A program may use at most 64 MiB of HBM per device.

v0:
```python
import math

import jax
import jax.numpy as jnp
from jax import lax
from jax.sharding import PartitionSpec as P

HEAD_DIM = 128


def shifted(value, axis, steps):
    count = lax.axis_size(axis)
    first, last = (max(0, -steps), min(count, count - steps))
    return lax.ppermute(value, axis, [(source, source + steps) for source in range(first, last)])


def body(queries, keys, values, doc_ids, out_weight):
    n_uly = lax.axis_size("uly")
    blk_index = lax.axis_index("blk")
    rows = queries.shape[0]
    head_dim = HEAD_DIM
    heads = queries.shape[1] // head_dim
    kv_heads = keys.shape[1] // head_dim
    repeat = max(1, n_uly // kv_heads)
    kv_local = max(n_uly, kv_heads) // n_uly
    local_heads = heads // n_uly
    grouped = local_heads // kv_local
    block = rows * n_uly
    sub_rows = math.gcd(block, 512)
    n_sub = block // sub_rows
    scale = 1.0 / math.sqrt(head_dim)
    query_ids = lax.all_gather(doc_ids, "uly", axis=0, tiled=True)
    query_split = queries.reshape(rows, heads, head_dim)
    key_wide = jnp.repeat(keys.reshape(rows, kv_heads, head_dim), repeat, axis=1)
    value_wide = jnp.repeat(values.reshape(rows, kv_heads, head_dim), repeat, axis=1)
    key_wide, value_wide = (key_wide, value_wide)
    query_local, key_local, value_local = (
        lax.all_to_all(query_split, "uly", split_axis=1, concat_axis=0, tiled=True),
        lax.all_to_all(key_wide, "uly", split_axis=1, concat_axis=0, tiled=True),
        lax.all_to_all(value_wide, "uly", split_axis=1, concat_axis=0, tiled=True),
    )
    carried = (key_local, value_local)
    query_grouped = query_local.reshape(n_sub, sub_rows, kv_local, grouped, head_dim)
    query_start = blk_index * block
    query_pos = query_start + jnp.arange(block, dtype=jnp.int32)
    first_id = query_ids[0]
    offsets = jnp.arange(block, dtype=jnp.int32)
    ids_sub = query_ids.reshape(n_sub, sub_rows)
    pos_sub = query_pos.reshape(n_sub, sub_rows)

    def attend(state, pair, key_ids, source):
        key_block, value_block = pair
        key_start = jnp.maximum(source, 0) * block
        key_pos = key_start + offsets
        needed = (source >= 0) & (
            (source == blk_index) | (source < blk_index) & (key_ids[block - 1] == first_id)
        )

        def compute(state_in):

            def one(item):
                query_part, pos_part, ids_part, accum, peak, total = item
                scores = (
                    jnp.einsum(
                        "qkgd,pkd->kgqp", query_part, key_block, preferred_element_type=jnp.float32
                    )
                    * scale
                )
                allowed = (key_pos[None, :] <= pos_part[:, None]) & (
                    key_ids[None, :] == ids_part[:, None]
                )
                scores = jnp.where(allowed, scores, -1e30)
                peak_new = jnp.maximum(peak, jnp.max(scores, axis=-1))
                expo = jnp.where(allowed, jnp.exp(scores - peak_new[..., None]), 0.0)
                factor = jnp.exp(peak - peak_new)
                total_new = total * factor + jnp.sum(expo, axis=-1)
                update = jnp.einsum(
                    "kgqp,pkd->kgqd",
                    expo.astype(jnp.bfloat16),
                    value_block,
                    preferred_element_type=jnp.float32,
                )
                return (accum * factor[..., None] + update, peak_new, total_new)

            return lax.map(
                one, (query_grouped, pos_sub, ids_sub, state_in[0], state_in[1], state_in[2])
            )

        def keep(state_in):
            return state_in

        return lax.cond(needed, compute, keep, state)

    start_state = (
        jnp.zeros((n_sub, kv_local, grouped, sub_rows, head_dim), jnp.float32),
        jnp.full((n_sub, kv_local, grouped, sub_rows), -1e30, jnp.float32),
        jnp.zeros((n_sub, kv_local, grouped, sub_rows), jnp.float32),
    )
    state = attend(start_state, carried, query_ids, blk_index)
    earlier_key, earlier_value, earlier_marks = shifted(
        (carried[0], carried[1], query_ids.astype(jnp.bfloat16)), "blk", 1
    )
    earlier_ids = earlier_marks.astype(jnp.int32)
    state = attend(state, (earlier_key, earlier_value), earlier_ids, blk_index - 1)
    accum, peak, total = state
    attn = (
        (accum / total[..., None])
        .transpose(0, 3, 1, 2, 4)
        .reshape(block, local_heads * head_dim)
        .astype(jnp.bfloat16)
    )
    mixed = lax.psum_scatter(
        jnp.dot(attn, out_weight, preferred_element_type=jnp.float32).astype(jnp.bfloat16),
        "uly",
        scatter_dimension=0,
        tiled=True,
    )
    return mixed


def solution(mesh):
    placed = (
        P(("blk", "uly"), None),
        P(("blk", "uly"), None),
        P(("blk", "uly"), None),
        P(("blk", "uly")),
        P("uly", None),
    )
    return jax.shard_map(
        body, mesh=mesh, in_specs=placed, out_specs=P(("blk", "uly"), None), check_vma=False
    )
```

profile of v0, /device:TPU:20, one launch (start us, length us, event | category | flops | bytes accessed | tf_op | source)
XLA Modules:
  0.0 183.6 jit_solution(14577532152778803910)
XLA Ops:
  6.5 0.0 copy-start
  6.5 1.8 copy.38
  8.3 5.2 %all-to-all-start.1 = ((bf16[128,8,128]{0,2,1:T(8,128)(2,1)}), bf16[128,8,128]{0,2,1:T(8,128)(2,1)S(1)}, u32[]{:S(2)}, u32[]{:S(2)}) async-start(bf16[128,8,128]{0,2,1:T(8,128)(2,1)} %bitcast.33), calls=%async_computation.1 | async-start | bytes 524288 | tf_op jit(solution)/shard_map/all_to_all | solution.py:39
  13.5 1.8 copy.41
  15.3 4.0 %all-to-all-done.1 = bf16[128,8,128]{0,2,1:T(8,128)(2,1)S(1)} async-done(((bf16[128,8,128]{0,2,1:T(8,128)(2,1)}), bf16[128,8,128]{0,2,1:T(8,128)(2,1)S(1)}, u32[]{:S(2)}, u32[]{:S(2)}) %all-to-all-start.1) | async-done | bytes 262176 | tf_op jit(solution)/shard_map/all_to_all | solution.py:39
  19.3 6.5 %all-to-all-start.2 = ((bf16[128,8,128]{0,2,1:T(8,128)(2,1)}), bf16[128,8,128]{0,2,1:T(8,128)(2,1)S(1)}, u32[]{:S(2)}, u32[]{:S(2)}) async-start(bf16[128,8,128]{0,2,1:T(8,128)(2,1)} %bitcast.38), calls=%async_computation.2 | async-start | bytes 524288 | tf_op jit(solution)/shard_map/all_to_all | solution.py:40
  25.8 1.6 copy.34
  27.5 1.3 copy.35
  28.8 1.7 all-to-all-done.2
  30.4 5.9 %all-to-all-start = ((bf16[128,32,128]{2,0,1:T(8,128)(2,1)}), bf16[128,32,128]{2,0,1:T(8,128)(2,1)S(1)}, u32[]{:S(2)}, u32[]{:S(2)}) async-start(bf16[128,32,128]{2,0,1:T(8,128)(2,1)} %copy.35), calls=%async_computation | async-start | bytes 2097152 | tf_op jit(solution)/shard_map/all_to_all | solution.py:38
  36.4 0.0 reduce-scatter.2.cloned.1.call-start
  36.4 0.8 copy.40
  37.2 0.9 copy.43
  38.1 1.9 %collective-permute-start.1 = (bf16[512,2,128]{2,0,1:T(8,128)(2,1)}, bf16[512,2,128]{2,0,1:T(8,128)(2,1)S(1)}, u32[]{:S(2)}, u32[]{:S(2)}) collective-permute-start(bf16[512,2,128]{2,0,1:T(8,128)(2,1)} %bitcast.37), channel_id=1, source_target_pairs={{0,4},{4,8},{8,12},{12,16},{16,20},{20,24},{24,28},{1,5},{5,9},{9,... | collective-permute-start | bytes 786440 | tf_op jit(solution)/shard_map/ppermute | solution.py:14
  40.0 3.5 %collective-permute-start.2 = (bf16[512,2,128]{2,0,1:T(8,128)(2,1)}, bf16[512,2,128]{2,0,1:T(8,128)(2,1)}, u32[]{:S(2)}, u32[]{:S(2)}) collective-permute-start(bf16[512,2,128]{2,0,1:T(8,128)(2,1)} %bitcast.42), channel_id=1, source_target_pairs={{0,4},{4,8},{8,12},{12,16},{16,20},{20,24},{24,28},{1,5},{5,9},{9,... | collective-permute-start | bytes 786440 | tf_op jit(solution)/shard_map/ppermute | solution.py:14
  43.5 0.0 copy-done
  43.5 16.5 %all-gather = s32[4,1,128]{2,1,0:T(1,128)S(1)} all-gather(s32[1,1,128]{2,1,0:T(1,128)S(1)} %bitcast.133), channel_id=1, replica_groups=mesh['blk'=8,'uly'=4] {'uly'}, dimensions={0}, use_global_device_ids=true | all-gather | bytes 2560 | tf_op jit(solution)/shard_map/all_gather | solution.py:32
  60.0 1.9 %collective-permute-start = (bf16[512]{0:T(512)(128)(2,1)S(1)}, bf16[512]{0:T(512)(128)(2,1)S(1)}, u32[]{:S(2)}, u32[]{:S(2)}) collective-permute-start(bf16[512]{0:T(512)(128)(2,1)S(1)} %convert_element_type.32), channel_id=1, source_target_pairs={{0,4},{4,8},{8,12},{12,16},{16,20},{20,24},{24,28},{1,5},{5,9},{9,... | collective-permute-start | bytes 3080 | tf_op jit(solution)/shard_map/ppermute | solution.py:14
  62.0 0.5 slice.7
  62.5 3.3 %collective-permute-done = bf16[512]{0:T(512)(128)(2,1)S(1)} collective-permute-done((bf16[512]{0:T(512)(128)(2,1)S(1)}, bf16[512]{0:T(512)(128)(2,1)S(1)}, u32[]{:S(2)}, u32[]{:S(2)}) %collective-permute-start) | collective-permute-done | bytes 1056 | tf_op jit(solution)/shard_map/ppermute | solution.py:14
  65.8 0.6 slice.6
  67.7 0.0 all-to-all-done
  67.7 0.1 copy.37
  67.8 8.8 %conditional.2 = (f32[1,2,4,512,128]{4,3,2,1,0:T(8,128)S(1)}, f32[1,2,4,512]{3,2,1,0:T(4,128)S(1)}, f32[1,2,4,512]{3,2,1,0:T(4,128)S(1)}) conditional(s32[]{:T(128)} %convert_element_type.35, () %tuple.24, (s32[]{:T(128)}, s32[512]{0:T(512)S(1)}, s32[1,512]{1,0:T(1,128)S(1)}, s32[512]{0:T(512)S(1)}, s32[1,512]{1,0:T(1,128)S(1)}, ...), branch_computations={%region_0.0_spmd, %region_1.4_spmd} | conditional | flops 1102336512 | bytes 30093364 | solution.py:92
  67.8 0.3 compare_and_fusion
  68.1 2.5 %fusion = (f32[2,4,512]{2,1,0:T(4,128)S(1)}, f32[2,512,512,4]{2,1,3,0:T(8,128)S(1)}) fusion(pred[512,512]{0,1:T(8,128)(4,1)S(1)} %compare_and_fusion, bf16[1,512,2,4,128]{4,1,3,2,0:T(8,128)(2,1)S(1)} %get-tuple-element.136, bf16[512,2,128]{2,0,1:T(8,128)(2,1)} %get-tuple-element.134), kind=kOutput, calls=%fused_computation.2 | convolution fusion | flops 543158272 | bytes 9977856 | tf_op jit(solution)/shard_map/cond/branch_1_fun/while/body/eval_jaxpr/qkgd,pkd->kgqp/dot_general | solution.py:64
  70.6 3.9 %add_bitcast_fusion = f32[1,2,4,512,128]{4,3,2,1,0:T(8,128)S(1)} fusion(f32[2,512,512,4]{2,1,3,0:T(8,128)S(1)} %get-tuple-element.172, f32[2,4,512]{2,1,0:T(4,128)S(1)} %get-tuple-element.170, pred[512,512]{0,1:T(8,128)(4,1)S(1)} %compare_and_fusion, f32[2,4,512]{2,1,0:T(4,128)S(1)} %get-tuple-element.169, bf16[512,2,128]{2,0,1:T(8,128)(2,1)} %get-tuple-element.138), kind=kOutput, calls=%fused_computation.7 | convolution fusion | flops 547880960 | bytes 11042816 | tf_op jit(solution)/shard_map/cond/branch_1_fun/while/body/eval_jaxpr/kgqp,pkd->kgqd/dot_general | solution.py:77
  74.5 2.0 %fusion.1 = f32[2,4,512]{2,1,0:T(4,128)S(1)} fusion(f32[2,512,512,4]{2,1,3,0:T(8,128)S(1)} %get-tuple-element.172, f32[2,4,512]{2,1,0:T(4,128)S(1)} %get-tuple-element.170, pred[512,512]{0,1:T(8,128)(4,1)S(1)} %compare_and_fusion), kind=kLoop, calls=%fused_computation.3 | loop fusion | flops 10481664 | bytes 8683520 | tf_op jit(solution)/shard_map/cond/branch_1_fun/while/body/eval_jaxpr/reduce_sum | solution.py:76
  76.6 0.0 collective-permute-done.1
  76.6 0.0 collective-permute-done.2
  76.6 12.1 %conditional.3 = (f32[1,2,4,512]{3,2,1,0:T(4,128)S(1)}, f32[1,2,4,512,128]{3,4,2,1,0:T(8,128)}) conditional(s32[]{:T(128)} %convert_element_type.34, (f32[1,2,4,512,128]{4,3,2,1,0:T(8,128)S(1)}, f32[1,2,4,512]{3,2,1,0:T(4,128)S(1)}) %tuple.26, (f32[1,2,4,512,128]{4,3,2,1,0:T(8,128)S(1)}, f32[1,2,4,512]{3,2,1,0:T(4,128)S(1)}, s32[]{:T(128)}, ...), branch_computations={%region_4.5_spmd, %region_5.8_spmd} | conditional | flops 1102856704 | bytes 36417580 | solution.py:92
  76.9 0.3 compare_and_fusion.1
  77.1 1.5 fusion.16
  78.7 2.0 %fusion.17 = f32[2,4,512]{2,1,0:T(4,128)S(1)} fusion(f32[2,512,512,4]{2,1,3,0:T(8,128)S(1)} %get-tuple-element.168, f32[2,4,512]{2,1,0:T(4,128)S(1)} %get-tuple-element.166, pred[512,512]{0,1:T(8,128)(4,1)S(1)} %compare_and_fusion.1), kind=kLoop, calls=%fused_computation.24 | loop fusion | flops 10481664 | bytes 8683520 | tf_op jit(solution)/shard_map/cond/branch_1_fun/while/body/eval_jaxpr/reduce_sum | solution.py:76
  80.8 5.0 %fusion.23 = f32[1,2,4,512,128]{4,3,2,1,0:T(8,128)} fusion(f32[1,2,4,512,128]{4,3,2,1,0:T(8,128)S(1)} %get-tuple-element.139, f32[2,512,512,4]{2,1,3,0:T(8,128)S(1)} %get-tuple-element.168, f32[2,4,512]{2,1,0:T(4,128)S(1)} %get-tuple-element.166, pred[512,512]{0,1:T(8,128)(4,1)S(1)} %compare_and_fusion.1, f32[2,4,512]{2,1,0:T(4,128)S(1)} %get-tuple-element.165, ...), kind=kOutput, calls=%fused_computation.30 | convolution fusion | flops 548405248 | bytes 13139968 | tf_op jit(solution)/shard_map/cond/branch_1_fun/while/body/eval_jaxpr/kgqp,pkd->kgqd/dot_general | solution.py:77
  85.8 2.9 %copy.55 = f32[1,2,4,512,128]{3,4,2,1,0:T(8,128)} copy(f32[1,2,4,512,128]{4,3,2,1,0:T(8,128)} %fusion.23) | data formatting | bytes 4194304 | tf_op jit(solution)/shard_map/cond | solution.py:92
  88.7 1.9 %divide_convert_fusion = bf16[1,2,4,512,128]{3,4,2,1,0:T(8,128)(2,1)S(1)} fusion(f32[1,2,4,512,128]{3,4,2,1,0:T(8,128)} %get-tuple-element.162, f32[2,4,512]{2,1,0:T(4,128)S(1)} %bitcast.122), kind=kLoop, calls=%fused_computation.48 | loop fusion | flops 1048576 | bytes 3162112 | tf_op jit(solution)/shard_map/convert_element_type | solution.py:110
  90.6 9.5 %convolution_convert_fusion = bf16[512,4096]{1,0:T(8,128)(2,1)} fusion(bf16[512,1024]{0,1:T(8,128)(2,1)S(1)} %bitcast.119, bf16[1024,4096]{1,0:T(8,128)(2,1)} %param.13), kind=kOutput, calls=%fused_computation.47 | convolution fusion | flops 4297064448 | bytes 13631488 | tf_op jit(solution)/shard_map/dot_general | solution.py:113
  100.1 0.0 reduce-scatter.2.cloned.1.call-update
  100.1 76.6 %reduce-scatter.2.cloned.1.call-done = bf16[128,4096]{1,0:T(8,128)(2,1)} async-done(((bf16[512,4096]{1,0:T(8,128)(2,1)}), bf16[128,4096]{1,0:T(8,128)(2,1)}) %reduce-scatter.2.cloned.1.call-update) | async-done | bytes 1048592 | tf_op jit(solution)/shard_map/reduce_scatter | solution.py:112
  (11 shorter events, 0.1 us)
Async XLA Ops:
  6.5 37.0 %copy-start = (s32[128]{0:T(128)S(1)}, s32[128]{0:T(128)}, u32[]{:S(2)}) copy-start(s32[128]{0:T(128)} %param.12) | copy-start | bytes 1540
  8.3 11.0 %all-to-all-start.1 = ((bf16[128,8,128]{0,2,1:T(8,128)(2,1)}), bf16[128,8,128]{0,2,1:T(8,128)(2,1)S(1)}, u32[]{:S(2)}, u32[]{:S(2)}) async-start(bf16[128,8,128]{0,2,1:T(8,128)(2,1)} %bitcast.33), calls=%async_computation.1 | async-start | bytes 524288 | tf_op jit(solution)/shard_map/all_to_all | solution.py:39
  19.3 11.1 %all-to-all-start.2 = ((bf16[128,8,128]{0,2,1:T(8,128)(2,1)}), bf16[128,8,128]{0,2,1:T(8,128)(2,1)S(1)}, u32[]{:S(2)}, u32[]{:S(2)}) async-start(bf16[128,8,128]{0,2,1:T(8,128)(2,1)} %bitcast.38), calls=%async_computation.2 | async-start | bytes 524288 | tf_op jit(solution)/shard_map/all_to_all | solution.py:40
  30.4 37.2 %all-to-all-start = ((bf16[128,32,128]{2,0,1:T(8,128)(2,1)}), bf16[128,32,128]{2,0,1:T(8,128)(2,1)S(1)}, u32[]{:S(2)}, u32[]{:S(2)}) async-start(bf16[128,32,128]{2,0,1:T(8,128)(2,1)} %copy.35), calls=%async_computation | async-start | bytes 2097152 | tf_op jit(solution)/shard_map/all_to_all | solution.py:38
  36.4 140.3 %reduce-scatter.2.cloned.1.call-start = ((), (), s32[]{:S(2)}) async-start(), calls=%async_computation.4 | async-start | bytes 5242880 | tf_op jit(solution)/shard_map/reduce_scatter | solution.py:112
  38.1 38.5 %collective-permute-start.1 = (bf16[512,2,128]{2,0,1:T(8,128)(2,1)}, bf16[512,2,128]{2,0,1:T(8,128)(2,1)S(1)}, u32[]{:S(2)}, u32[]{:S(2)}) collective-permute-start(bf16[512,2,128]{2,0,1:T(8,128)(2,1)} %bitcast.37), channel_id=1, source_target_pairs={{0,4},{4,8},{8,12},{12,16},{16,20},{20,24},{24,28},{1,5},{5,9},{9,... | collective-permute-start | bytes 786440 | tf_op jit(solution)/shard_map/ppermute | solution.py:14
  40.0 36.6 %collective-permute-start.2 = (bf16[512,2,128]{2,0,1:T(8,128)(2,1)}, bf16[512,2,128]{2,0,1:T(8,128)(2,1)}, u32[]{:S(2)}, u32[]{:S(2)}) collective-permute-start(bf16[512,2,128]{2,0,1:T(8,128)(2,1)} %bitcast.42), channel_id=1, source_target_pairs={{0,4},{4,8},{8,12},{12,16},{16,20},{20,24},{24,28},{1,5},{5,9},{9,... | collective-permute-start | bytes 786440 | tf_op jit(solution)/shard_map/ppermute | solution.py:14
  60.0 5.8 %collective-permute-start = (bf16[512]{0:T(512)(128)(2,1)S(1)}, bf16[512]{0:T(512)(128)(2,1)S(1)}, u32[]{:S(2)}, u32[]{:S(2)}) collective-permute-start(bf16[512]{0:T(512)(128)(2,1)S(1)} %convert_element_type.32), channel_id=1, source_target_pairs={{0,4},{4,8},{8,12},{12,16},{16,20},{20,24},{24,28},{1,5},{5,9},{9,... | collective-permute-start | bytes 3080 | tf_op jit(solution)/shard_map/ppermute | solution.py:14
Sparse Core Ops, SparseCore 0:
  100.2 76.4 reduce-scatter.1
where the time goes:
time: 185 us; the launch traced here: 184 us
  waiting for transfers between devices  85.6 us (46%)
  starting transfers between devices  24.9 us (13%)
  matrix products  22.5 us (12%)
  blocking collectives  16.5 us (9%)
  between operations  14.7 us (8%)
  local copies, waits for them, and re-layouts  12.3 us (7%)
  other arithmetic  6.62 us (4%)
    reduce_scatter x1, waiting for transfers between devices, body(): lax.psum_scatter(jnp.dot(attn, out_weight, preferred_element_type=jnp.flo...  76.6 us
    all_gather x1, blocking collectives, body(): query_ids = lax.all_gather(doc_ids, 'uly', axis=0, tiled=True)  16.5 us
    dot_general x1, matrix products, body(): jnp.dot(attn, out_weight, preferred_element_type=jnp.float32)  9.49 us
    dot_general x2, matrix products, one(): jnp.einsum('kgqp,pkd->kgqd', expo.astype(jnp.bfloat16), value_block, pref...  8.96 us
    ppermute x3, starting transfers between devices, shifted(): lax.ppermute(value, axis, [(source, source + steps) for source in range(f...  7.32 us
    all_to_all x1, starting transfers between devices, body(): lax.all_to_all(value_wide, 'uly', split_axis=1, concat_axis=0, tiled=True)  6.48 us
    all_to_all x1, starting transfers between devices, body(): lax.all_to_all(query_split, 'uly', split_axis=1, concat_axis=0, tiled=True)  5.91 us
    all_to_all x1, starting transfers between devices, body(): lax.all_to_all(key_wide, 'uly', split_axis=1, concat_axis=0, tiled=True)  5.2 us
  transfers between devices with their start and end apart: 7, of which 4 were waited for; matrix products, arithmetic and copies ran while one was open for 9% of the time, Pallas kernels for 0%

commit v1 on v0

v1 whole, which is shorter than its diff:
```python
import functools
import math

import jax
import jax.numpy as jnp
from jax import lax
from jax.experimental import pallas as pl
from jax.experimental.pallas import tpu as pltpu
from jax.sharding import PartitionSpec as P

HEAD_DIM = 128
MESH = pl.DeviceIdType.MESH
PIECES = 8


def kernel(n, n_blk, heads, kv_heads, q_ref, k_ref, v_ref, id_ref, w_ref, o_ref,
           qbuf, kbuf, vbuf, idbuf, wbuf, attn, run,
           send_sem, recv_sem, halo_send, halo_recv, run_send, run_recv, w_sem):
    me = lax.axis_index("uly")
    blk = lax.axis_index("blk")
    hd = HEAD_DIM
    rows = q_ref.shape[0]
    block = rows * n
    local_heads = heads // n
    kv_local = max(n, kv_heads) // n
    grouped = local_heads // kv_local
    q_width = local_heads * hd
    kv_width = kv_local * hd
    piece_cols = w_ref.shape[1] // PIECES
    scale = 1.0 / math.sqrt(hd)
    window = n + 1

    def q_cols(dev):
        return pl.ds(pl.multiple_of(dev * q_width, 128), q_width)

    def kv_cols(dev):
        return pl.ds(pl.multiple_of((dev * kv_heads) // n * hd, 128), kv_width)

    w_copy = pltpu.make_async_copy(w_ref, wbuf, w_sem)
    w_copy.start()

    barrier = pltpu.get_barrier_semaphore()
    for off in range(1, n):
        peer = lax.rem(me + off, n)
        pl.semaphore_signal(barrier, inc=1, device_id={"uly": peer}, device_id_type=MESH)

    @pl.when(blk > 0)
    def _():
        pl.semaphore_signal(barrier, inc=1, device_id={"blk": blk - 1}, device_id_type=MESH)

    @pl.when(blk < n_blk - 1)
    def _():
        pl.semaphore_signal(barrier, inc=1, device_id={"blk": blk + 1}, device_id_type=MESH)

    def own_copies():
        return (
            pltpu.make_async_copy(k_ref.at[:, kv_cols(me)], kbuf.at[n + me], recv_sem.at[0, me]),
            pltpu.make_async_copy(v_ref.at[:, kv_cols(me)], vbuf.at[n + me], recv_sem.at[1, me]),
            pltpu.make_async_copy(id_ref, idbuf.at[n + me], recv_sem.at[2, me]),
            pltpu.make_async_copy(q_ref.at[:, q_cols(me)], qbuf.at[me], recv_sem.at[3, me]),
        )

    for copy in own_copies():
        copy.start()

    @pl.when(blk == 0)
    def _():
        kbuf[0:n] = jnp.zeros((n, rows, kv_width), kbuf.dtype)
        vbuf[0:n] = jnp.zeros((n, rows, kv_width), vbuf.dtype)
        idbuf[0:n] = jnp.full((n, 1, rows), -1, jnp.int32)

    pl.semaphore_wait(barrier, n - 1 + jnp.where(blk > 0, 1, 0) + jnp.where(blk < n_blk - 1, 1, 0))

    def remote(src, dst, kind, dev):
        return pltpu.make_async_remote_copy(
            src_ref=src, dst_ref=dst, send_sem=send_sem.at[kind, dev], recv_sem=recv_sem.at[kind, me],
            device_id={"uly": dev}, device_id_type=MESH)

    def kv_sends(dev):
        return (
            remote(id_ref, idbuf.at[n + me], 2, dev),
            remote(k_ref.at[:, kv_cols(dev)], kbuf.at[n + me], 0, dev),
            remote(v_ref.at[:, kv_cols(dev)], vbuf.at[n + me], 1, dev),
        )

    def q_send(dev):
        return remote(q_ref.at[:, q_cols(dev)], qbuf.at[me], 3, dev)

    def each_peer(run_on):
        for off in range(n - 1, 0, -1):
            for dev in (me + off, me - off):
                pl.when((dev >= 0) & (dev < n))(functools.partial(run_on, dev))

    def start_kv(dev):
        for copy in kv_sends(dev):
            copy.start()

    each_peer(start_kv)
    each_peer(lambda dev: q_send(dev).start())

    def halo(slot):
        def one(kind, buf):
            return pltpu.make_async_remote_copy(
                src_ref=buf.at[n + slot], dst_ref=buf.at[slot],
                send_sem=halo_send.at[kind, slot], recv_sem=halo_recv.at[kind, slot],
                device_id={"blk": blk + 1}, device_id_type=MESH)
        return (one(0, kbuf), one(1, vbuf), one(2, idbuf))

    def arrive(slot):
        for kind, buf in ((2, idbuf), (0, kbuf), (1, vbuf)):
            pltpu.make_async_copy(buf.at[n + slot], buf.at[n + slot], recv_sem.at[kind, slot]).wait()

        @pl.when(blk < n_blk - 1)
        def _():
            for copy in halo(slot):
                copy.start()

    arrive(me)
    for off in range(1, n):
        for dev in (me + off, me - off):
            pl.when((dev >= 0) & (dev < n))(functools.partial(arrive, dev))

    @pl.when(blk > 0)
    def _():
        for slot in range(n):
            for copy in halo(slot):
                copy.wait_recv()

    w_copy.wait()

    def attend(d):
        pltpu.make_async_copy(qbuf.at[d], qbuf.at[d], recv_sem.at[3, d]).wait()
        key_ids = jnp.concatenate([idbuf[d + i] for i in range(window)], axis=1)
        query_ids = jnp.broadcast_to(idbuf[n + d], (rows, rows)).T[:, :1]
        col = lax.broadcasted_iota(jnp.int32, (rows, window * rows), 1)
        row = lax.broadcasted_iota(jnp.int32, (rows, window * rows), 0)
        allowed = (key_ids == query_ids) & (col <= row + block)
        for g in range(kv_local):
            key = kbuf[pl.ds(d, window), :, g * hd:(g + 1) * hd].reshape(window * rows, hd)
            value = vbuf[pl.ds(d, window), :, g * hd:(g + 1) * hd].reshape(window * rows, hd)
            for r in range(grouped):
                h = g * grouped + r
                query = qbuf[d, :, h * hd:(h + 1) * hd]
                scores = lax.dot_general(query, key, (((1,), (1,)), ((), ())),
                                         preferred_element_type=jnp.float32) * scale
                scores = jnp.where(allowed, scores, -1e30)
                peak = jnp.max(scores, axis=-1, keepdims=True)
                expo = jnp.exp(scores - peak)
                total = jnp.sum(expo, axis=-1, keepdims=True)
                summed = jnp.dot(expo.astype(jnp.bfloat16), value, preferred_element_type=jnp.float32)
                attn[d, :, h * hd:(h + 1) * hd] = (summed / total).astype(jnp.bfloat16)

    def part(d, p):
        cols = pl.ds(pl.multiple_of(p * piece_cols, 128), piece_cols)
        return jnp.dot(attn[d], wbuf[:, cols], preferred_element_type=jnp.float32)

    def hop(way, d, p, dev):
        return pltpu.make_async_remote_copy(
            src_ref=run.at[way, d, p], dst_ref=run.at[way, d, p],
            send_sem=run_send.at[way, d, p], recv_sem=run_recv.at[way, d, p],
            device_id={"uly": dev}, device_id_type=MESH)

    def landed(way, d, p):
        pltpu.make_async_copy(run.at[way, d, p], run.at[way, d, p], run_recv.at[way, d, p]).wait()

    def pass_on(d, p):
        way = jnp.where(d > me, 0, 1)
        dev = jnp.where(d > me, me + 1, me - 1)
        first = jnp.where(d > me, me, n - 1 - me) == 0
        acc = part(d, p)

        @pl.when(first)
        def _():
            run[way, d, p] = acc.astype(jnp.bfloat16)

        @pl.when(jnp.logical_not(first))
        def _():
            landed(way, d, p)
            run[way, d, p] = (acc + run[way, d, p].astype(jnp.float32)).astype(jnp.bfloat16)

        hop(way, d, p, dev).start()

    def pair(t, carry):
        far, near = n - 1 - t, t
        attend(far)
        attend(near)

        def step(p, inner):
            pl.when(far != me)(functools.partial(pass_on, far, p))
            pl.when(near != me)(functools.partial(pass_on, near, p))
            return inner

        return lax.fori_loop(0, PIECES, step, carry)

    lax.fori_loop(0, n // 2, pair, 0)

    def finish(p, carry):
        cols = pl.ds(pl.multiple_of(p * piece_cols, 128), piece_cols)
        run_sum = part(me, p)
        wbufless = run_sum

        @pl.when(me == 0)
        def _():
            landed(1, me, p)
            o_ref[:, cols] = (wbufless + run[1, me, p].astype(jnp.float32)).astype(o_ref.dtype)

        @pl.when(me == n - 1)
        def _():
            landed(0, me, p)
            o_ref[:, cols] = (wbufless + run[0, me, p].astype(jnp.float32)).astype(o_ref.dtype)

        @pl.when((me > 0) & (me < n - 1))
        def _():
            landed(0, me, p)
            landed(1, me, p)
            both = run[0, me, p].astype(jnp.float32) + run[1, me, p].astype(jnp.float32)
            o_ref[:, cols] = (wbufless + both).astype(o_ref.dtype)

        return carry

    lax.fori_loop(0, PIECES, finish, 0)

    def end_peer(dev):
        for copy in kv_sends(dev):
            copy.wait_send()
        q_send(dev).wait_send()

    each_peer(end_peer)

    @pl.when(blk < n_blk - 1)
    def _():
        for slot in range(n):
            for copy in halo(slot):
                copy.wait_send()

    def end_run(i, carry):
        d, p = i // PIECES, lax.rem(i, PIECES)

        @pl.when(d != me)
        def _():
            hop(jnp.where(d > me, 0, 1), d, p, jnp.where(d > me, me + 1, me - 1)).wait_send()

        return carry

    lax.fori_loop(0, n * PIECES, end_run, 0)


def body(queries, keys, values, doc_ids, out_weight):
    n = lax.axis_size("uly")
    n_blk = lax.axis_size("blk")
    rows = queries.shape[0]
    hd = HEAD_DIM
    heads = queries.shape[1] // hd
    kv_heads = keys.shape[1] // hd
    kv_width = max(n, kv_heads) // n * hd
    q_width = heads // n * hd
    out_cols = out_weight.shape[1]
    vmem = pl.BlockSpec(memory_space=pltpu.VMEM)
    return pl.pallas_call(
        functools.partial(kernel, n, n_blk, heads, kv_heads),
        out_shape=jax.ShapeDtypeStruct((rows, out_cols), jnp.bfloat16),
        in_specs=[vmem] * 4 + [pl.BlockSpec(memory_space=pl.ANY)],
        out_specs=vmem,
        scratch_shapes=[
            pltpu.VMEM((n, rows, q_width), jnp.bfloat16),
            pltpu.VMEM((2 * n, rows, kv_width), jnp.bfloat16),
            pltpu.VMEM((2 * n, rows, kv_width), jnp.bfloat16),
            pltpu.VMEM((2 * n, 1, rows), jnp.int32),
            pltpu.VMEM(out_weight.shape, jnp.bfloat16),
            pltpu.VMEM((n, rows, q_width), jnp.bfloat16),
            pltpu.VMEM((2, n, PIECES, rows, out_cols // PIECES), jnp.bfloat16),
            pltpu.SemaphoreType.DMA((4, n)),
            pltpu.SemaphoreType.DMA((4, n)),
            pltpu.SemaphoreType.DMA((3, n)),
            pltpu.SemaphoreType.DMA((3, n)),
            pltpu.SemaphoreType.DMA((2, n, PIECES)),
            pltpu.SemaphoreType.DMA((2, n, PIECES)),
            pltpu.SemaphoreType.DMA,
        ],
        compiler_params=pltpu.CompilerParams(
            collective_id=0, has_side_effects=True, vmem_limit_bytes=60 * 1024 * 1024
        ),
    )(queries, keys, values, doc_ids.reshape(1, rows), out_weight)


def solution(mesh):
    placed = (
        P(("blk", "uly"), None),
        P(("blk", "uly"), None),
        P(("blk", "uly"), None),
        P(("blk", "uly")),
        P("uly", None),
    )
    return jax.shard_map(
        body, mesh=mesh, in_specs=placed, out_specs=P(("blk", "uly"), None), check_vma=False
    )
```

time: 185 us -> 138 us (0.75)
  Pallas kernels: 0 us -> 136 us
  waiting for transfers between devices: 85.6 us -> 0 us
  starting transfers between devices: 24.9 us -> 0 us
  matrix products: 22.5 us -> 0 us
  blocking collectives: 16.5 us -> 0 us
  between operations: 14.7 us -> 0.01 us
  local copies, waits for them, and re-layouts: 12.3 us -> 2.29 us
  other arithmetic: 6.62 us -> 0 us
    pallas_call x0 -> x1, Pallas kernels: none -> 136 us  [body(): pl.pallas_call(functools.partial(kernel, n, n_blk, heads, kv_heads), out_...]
    reduce_scatter x1 -> x0, waiting for transfers between devices: 76.6 us -> none  [body(): lax.psum_scatter(jnp.dot(attn, out_weight, preferred_element_type=jnp.flo...]
    dot_general x5 -> x0, matrix products: 22.5 us -> none  [the longest x1 9.49 us: body(): jnp.dot(attn, out_weight, preferred_element_type=jnp.float32)]
    all_to_all x3 -> x0, starting transfers between devices: 17.6 us -> none  [the longest x1 6.48 us: body(): lax.all_to_all(value_wide, 'uly', split_axis=1, concat_axis=0, tiled=True)]
    all_gather x1 -> x0, blocking collectives: 16.5 us -> none  [body(): query_ids = lax.all_gather(doc_ids, 'uly', axis=0, tiled=True)]
    ppermute x3 -> x0, starting transfers between devices: 7.32 us -> none  [shifted(): lax.ppermute(value, axis, [(source, source + steps) for source in range(f...]
    all_to_all x3 -> x0, waiting for transfers between devices: 5.71 us -> none  [the longest x1 4.02 us: body(): lax.all_to_all(key_wide, 'uly', split_axis=1, concat_axis=0, tiled=True)]
    reduce_sum x2 -> x0, other arithmetic: 4.1 us -> none  [one(): total_new = total * factor + jnp.sum(expo, axis=-1)]
  transfers between devices with their start and end apart: 7 -> 0, of which waited for: 4 -> 0; matrix products, arithmetic and copies ran while one was open for 9% -> 0% of each run, Pallas kernels for 0% -> 0%
where the time goes in v1:
time: 138 us
  Pallas kernels  136 us (99%)
  local copies, waits for them, and re-layouts  2.29 us (2%)
    pallas_call x1, Pallas kernels, body(): pl.pallas_call(functools.partial(kernel, n, n_blk, heads, kv_heads), out_...  136 us

profile of v1, /device:TPU:20, one launch (start us, length us, event | category | flops | bytes accessed | tf_op | source)
XLA Modules:
  0.0 138.1 jit_solution(6185216559045510730)
XLA Ops:
  0.0 135.8 %shard_map.55 = bf16[128,4096]{1,0:T(8,128)(2,1)} custom-call(bf16[128,4096]{1,0:T(8,128)(2,1)} %q_ref.1, bf16[128,1024]{1,0:T(8,128)(2,1)} %k_ref.1, bf16[128,1024]{1,0:T(8,128)(2,1)} %v_ref.1, s32[1,128]{1,0:T(1,128)} %bitcast.1, bf16[1024,4096]{1,0:T(8,128)(2,1)} %w_ref.1), custom_call_target="tpu_custom_call" | custom-call | tf_op jit(solution)/shard_map/pallas_call | solution.py:259
  135.8 2.3 %copy.7 = bf16[128,4096]{1,0:T(8,128)(2,1)} copy(bf16[128,4096]{1,0:T(8,128)(2,1)} %shard_map.55) | data formatting | bytes 2097152

commit v2 on v1

--- a/solution.py
+++ b/solution.py
@@ -96,7 +96,10 @@
             copy.start()
 
     each_peer(start_kv)
-    each_peer(lambda dev: q_send(dev).start())
+    for i in range(n):
+        place = n - 1 - i // 2 if i % 2 == 0 else i // 2
+        dev = jnp.where(me < n // 2, place, n - 1 - place)
+        pl.when(dev != me)(lambda dev=dev: q_send(dev).start())
 
     def halo(slot):
         def one(kind, buf):
@@ -180,41 +183,49 @@
 
         hop(way, d, p, dev).start()
 
+    low = me < n // 2
+    end = (me == 0) | (me == n - 1)
+
     def pair(t, carry):
-        far, near = n - 1 - t, t
-        attend(far)
-        attend(near)
-
-        def step(p, inner):
-            pl.when(far != me)(functools.partial(pass_on, far, p))
-            pl.when(near != me)(functools.partial(pass_on, near, p))
-            return inner
-
-        return lax.fori_loop(0, PIECES, step, carry)
+        one = jnp.where(low, n - 1 - t, t)
+        two = n - 1 - one
+
+        def pieces(which):
+            def step(p, inner):
+                for d in which:
+                    pl.when(d != me)(functools.partial(pass_on, d, p))
+                return inner
+            lax.fori_loop(0, PIECES, step, 0)
+
+        attend(one)
+        pl.when(end)(functools.partial(pieces, (one,)))
+        attend(two)
+        pl.when(end)(functools.partial(pieces, (two,)))
+        pl.when(jnp.logical_not(end))(functools.partial(pieces, (one, two)))
+        return carry
 
     lax.fori_loop(0, n // 2, pair, 0)
 
     def finish(p, carry):
         cols = pl.ds(pl.multiple_of(p * piece_cols, 128), piece_cols)
-        run_sum = part(me, p)
-        wbufless = run_sum
+        own = part(me, p)
 
         @pl.when(me == 0)
         def _():
             landed(1, me, p)
-            o_ref[:, cols] = (wbufless + run[1, me, p].astype(jnp.float32)).astype(o_ref.dtype)
+            o_ref[:, cols] = (own + run[1, me, p].astype(jnp.float32)).astype(o_ref.dtype)
 
         @pl.when(me == n - 1)
         def _():
             landed(0, me, p)
-            o_ref[:, cols] = (wbufless + run[0, me, p].astype(jnp.float32)).astype(o_ref.dtype)
+            o_ref[:, cols] = (own + run[0, me, p].astype(jnp.float32)).astype(o_ref.dtype)
 
         @pl.when((me > 0) & (me < n - 1))
         def _():
             landed(0, me, p)
             landed(1, me, p)
             both = run[0, me, p].astype(jnp.float32) + run[1, me, p].astype(jnp.float32)
-            o_ref[:, cols] = (wbufless + both).astype(o_ref.dtype)
+            o_ref[:, cols] = (own + both).astype(o_ref.dtype)
 
         return carry
 

time: 138 us -> 108 us (0.78); the launches traced: 138 us -> 106 us
  Pallas kernels: 136 us -> 104 us
    pallas_call x1, Pallas kernels: 136 us -> 104 us  [body(): pl.pallas_call(functools.partial(kernel, n, n_blk, heads, kv_heads), out_...]
where the time goes in v2:
time: 108 us; the launch traced here: 106 us
  Pallas kernels  104 us (96%)
  local copies, waits for them, and re-layouts  2.29 us (2%)
    pallas_call x1, Pallas kernels, body(): pl.pallas_call(functools.partial(kernel, n, n_blk, heads, kv_heads), out_...  104 us
    unnamed x1, local copies, waits for them, and re-layouts  2.29 us

profile of v2, /device:TPU:20, one launch (start us, length us, event | category | flops | bytes accessed | tf_op | source)
XLA Modules:
  0.0 106.4 jit_solution(1940933938992509751)
XLA Ops:
  0.0 104.1 %shard_map.55 = bf16[128,4096]{1,0:T(8,128)(2,1)} custom-call(bf16[128,4096]{1,0:T(8,128)(2,1)} %q_ref.1, bf16[128,1024]{1,0:T(8,128)(2,1)} %k_ref.1, bf16[128,1024]{1,0:T(8,128)(2,1)} %v_ref.1, s32[1,128]{1,0:T(1,128)} %bitcast.1, bf16[1024,4096]{1,0:T(8,128)(2,1)} %w_ref.1), custom_call_target="tpu_custom_call" | custom-call | tf_op jit(solution)/shard_map/pallas_call | solution.py:270
  104.1 2.3 %copy.7 = bf16[128,4096]{1,0:T(8,128)(2,1)} copy(bf16[128,4096]{1,0:T(8,128)(2,1)} %shard_map.55) | data formatting | bytes 2097152

commit v3 on v2

--- a/solution.py
+++ b/solution.py
@@ -10,7 +10,7 @@
 
 HEAD_DIM = 128
 MESH = pl.DeviceIdType.MESH
-PIECES = 8
+PIECES = 4
 
 
 def kernel(n, n_blk, heads, kv_heads, q_ref, k_ref, v_ref, id_ref, w_ref, o_ref,

time: 108 us -> 104 us (0.963)
  Pallas kernels: 104 us -> 101 us
    pallas_call x1, Pallas kernels: 104 us -> 101 us  [body(): pl.pallas_call(functools.partial(kernel, n, n_blk, heads, kv_heads), out_...]
where the time goes in v3:
time: 104 us; the launch traced here: 103 us
  Pallas kernels  101 us (97%)
  local copies, waits for them, and re-layouts  2.29 us (2%)
    pallas_call x1, Pallas kernels, body(): pl.pallas_call(functools.partial(kernel, n, n_blk, heads, kv_heads), out_...  101 us
    unnamed x1, local copies, waits for them, and re-layouts  2.29 us

profile of v3, /device:TPU:20, one launch (start us, length us, event | category | flops | bytes accessed | tf_op | source)
XLA Modules:
  0.0 102.9 jit_solution(9852626923638866088)
XLA Ops:
  0.0 100.6 %shard_map.55 = bf16[128,4096]{1,0:T(8,128)(2,1)} custom-call(bf16[128,4096]{1,0:T(8,128)(2,1)} %q_ref.1, bf16[128,1024]{1,0:T(8,128)(2,1)} %k_ref.1, bf16[128,1024]{1,0:T(8,128)(2,1)} %v_ref.1, s32[1,128]{1,0:T(1,128)} %bitcast.1, bf16[1024,4096]{1,0:T(8,128)(2,1)} %w_ref.1), custom_call_target="tpu_custom_call" | custom-call | tf_op jit(solution)/shard_map/pallas_call | solution.py:270
  100.6 2.3 %copy.7 = bf16[128,4096]{1,0:T(8,128)(2,1)} copy(bf16[128,4096]{1,0:T(8,128)(2,1)} %shard_map.55) | data formatting | bytes 2097152
